TPU v7x, 32 devices: a whole 2x2x4 slice. The times are simulated.
32 devices in a mesh: groups: 2 (over x), rows: 16 (over z, y, core).
Axes of the slice: x: 2, y: 2, z: 4, core: 2. Of those that a mesh axis runs over, the one named last changes fastest.
Arguments:
- slide_band: bfloat16 [96, 256, 512], P(None, ('groups', 'rows')), parts along dimension 1, may hold values from -8 to 8
- tissue_flags: int32 [32, 64], P(('groups', 'rows')), parts along dimension 0, may hold values from 0 to 1, as said below
- stain_index: int32 [32, 64], P(('groups', 'rows')), parts along dimension 0, may hold values from 0 to 3
- stain_gain: float32 [4, 96], replicated, may hold values from 0.5 to 2
- conv_weights: bfloat16 [3, 9, 96, 96], replicated, may hold values from -0.21875 to 0.21875
- norm_gain: float32 [3, 96], replicated, may hold values from 0.5 to 2
- norm_bias: float32 [3, 96], replicated, may hold values from -3 to 3
Outputs:
- features: bfloat16 [96, 256, 512], P(None, ('groups', 'rows')), parts along dimension 1
There are 2 independent parts, one for each index of `groups`. A program takes and returns all parts, laid end to end along the dimension named above; an argument that names none is the same for every part. Nothing has to cross between parts.
Inputs may be any that keep to these rules, and one draw needn't show every extreme that they name: `tissue_flags`: in every aligned block of 1 tile rows, the first tile of the block's first tile row is tissue.
All inputs are finite; a program needn't handle non-finite values.
Results may differ from a plain program's by a relative error of at most 0.018.
Values may be sent and summed in bfloat16 or wider, within the bound.
A program may use at most 64 MiB of HBM per device.

v0:
```python
import jax
import jax.numpy as jnp
from jax import lax
from jax.sharding import PartitionSpec as P

LAYERS = 3
TILE = 8
STAINS = 4


epsilon = 1e-05


def with_halo(cells, sides, width):
    for axis, dim in sides:
        count = lax.axis_size(axis)
        ends = count - 1
        head = lax.slice_in_dim(cells, 0, width, axis=dim)
        tail = lax.slice_in_dim(cells, cells.shape[dim] - width, cells.shape[dim], axis=dim)
        cells = jnp.concatenate(
            [
                lax.ppermute(tail, axis, [(i, (i + 1) % count) for i in range(ends)]),
                cells,
                lax.ppermute(head, axis, [((i + 1) % count, i) for i in range(ends)]),
            ],
            axis=dim,
        )
    return cells


def spread_tiles(tiles):
    shape = tiles.shape
    leading = shape[:-2]
    tile_rows = shape[-2]
    tile_cols = shape[-1]
    widened = jnp.broadcast_to(
        tiles[..., :, None, :, None], leading + (tile_rows, TILE, tile_cols, TILE)
    )
    return widened.reshape(leading + (tile_rows * TILE, tile_cols * TILE))


def dilated(inputs, weights, spacing, out_rows):
    col_count = inputs.shape[2]
    padded = jnp.pad(inputs, ((0, 0), (0, 0), (spacing, spacing)))
    running = None
    for kernel_tap in range(9):
        row_tap = kernel_tap // 3
        col_tap = kernel_tap % 3
        window = padded[
            :,
            row_tap * spacing : row_tap * spacing + out_rows,
            col_tap * spacing : col_tap * spacing + col_count,
        ]
        product = jnp.dot(
            weights[kernel_tap],
            window.reshape(inputs.shape[0], -1),
            preferred_element_type=jnp.float32,
        )
        running = product if kernel_tap == 0 else running + product
    return running.reshape(weights.shape[1], out_rows, col_count)


def statistics(own_response, own_pixels):
    masked = own_response * own_pixels[None]
    sums_all, squares_all, count_all = lax.psum(
        (
            jnp.sum(masked, axis=(1, 2)),
            jnp.sum(masked * own_response, axis=(1, 2)),
            jnp.sum(own_pixels),
        ),
        "rows",
    )
    average = sums_all / count_all
    variance = squares_all / count_all - average * average
    return (average, variance)


def finish(response, average, variance, gain_row, bias_row, row_pixels):
    centred = response - average[:, None, None]
    scaled = (
        gain_row[:, None, None] * centred * lax.rsqrt(variance + epsilon)[:, None, None]
        + bias_row[:, None, None]
    )
    return (jnp.maximum(scaled, 0.0) * row_pixels[None]).astype(jnp.bfloat16)


def per_device(
    slide_band, tissue_flags, stain_index, stain_gain, conv_weights, norm_gain, norm_bias
):
    one_hot = (
        stain_index[:, :, None] == jnp.arange(STAINS, dtype=jnp.int32)[None, None, :]
    ).astype(jnp.float32)
    per_tile = jnp.einsum("rcs,sk->krc", one_hot, stain_gain)
    stain_scale = spread_tiles(per_tile)
    pixels = spread_tiles(tissue_flags.astype(jnp.float32))
    current = (slide_band.astype(jnp.float32) * stain_scale * pixels[None]).astype(jnp.bfloat16)
    own_rows = slide_band.shape[1]
    for layer_index in range(LAYERS):
        spacing = 2**layer_index
        padded = with_halo(current, (("rows", 1),), spacing)
        response = dilated(padded, conv_weights[layer_index], spacing, own_rows)
        average, variance = statistics(response, pixels)
        current = finish(
            response, average, variance, norm_gain[layer_index], norm_bias[layer_index], pixels
        )
    return current


def solution(mesh):
    in_specs = (
        P(None, ("groups", "rows"), None),
        P(("groups", "rows"), None),
        P(("groups", "rows"), None),
        P(),
        P(),
        P(),
        P(),
    )
    out_specs = P(None, ("groups", "rows"), None)
    return jax.shard_map(
        per_device, mesh=mesh, in_specs=in_specs, out_specs=out_specs, check_vma=False
    )
```

profile of v0, /device:TPU:0, one launch (start us, length us, event | category | flops | bytes accessed | tf_op | source)
XLA Modules:
  0.0 144.5 jit_solution(7490979190416185358)
XLA Ops:
  0.0 0.7 convert_bitcast_fusion
  0.9 0.8 convolution_bitcast_fusion
  1.9 1.4 multiply_convert_fusion
  3.4 2.4 %collective-permute-start = (bf16[96,1,512]{2,0,1:T(8,128)(2,1)S(1)}, bf16[96,1,512]{2,0,1:T(8,128)(2,1)S(1)}, u32[]{:S(2)}, u32[]{:S(2)}) collective-permute-start(bf16[96,1,512]{2,0,1:T(8,128)(2,1)S(1)} %get-tuple-element.52), channel_id=1, source_target_pairs={{0,1},{1,2},{2,3},{3,4},{4,5},{5,6},{6,7},{7,8},{8,9},{9,10},{10,1... | collective-permute-start | bytes 294920 | tf_op jit(solution)/shard_map/ppermute | solution.py:22
  5.8 1.3 collective-permute-start.1
  8.1 3.0 %collective-permute-done.1 = bf16[96,1,512]{2,0,1:T(8,128)(2,1)S(1)} collective-permute-done((bf16[96,1,512]{2,0,1:T(8,128)(2,1)S(1)}, bf16[96,1,512]{2,0,1:T(8,128)(2,1)S(1)}, u32[]{:S(2)}, u32[]{:S(2)}) %collective-permute-start.1) | collective-permute-done | bytes 98336 | tf_op jit(solution)/shard_map/ppermute | solution.py:24
  12.1 1.1 slice_bitcast_fusion.12
  13.6 0.9 copy-done.3
  18.1 33.4 %all-reduce.5 = (f32[96]{0:T(128)S(1)}, f32[]{:T(128)}, f32[96]{0:T(128)S(1)}) all-reduce(f32[96]{0:T(128)S(1)} %get-tuple-element.10, f32[]{:T(128)} %get-tuple-element.60, f32[96]{0:T(128)S(1)} %get-tuple-element.9), channel_id=1, replica_groups=mesh['groups'=2,'rows'=16] {'rows'}, use_global_device_ids=true, to_apply=%region_1.2 | all-reduce | flops 193 | bytes 1544 | tf_op jit(solution)/shard_map/psum | solution.py:65
  52.7 1.3 collective-permute-start.2
  54.0 1.5 %collective-permute-start.3 = (bf16[96,2,512]{2,0,1:T(8,128)(2,1)S(1)}, bf16[96,2,512]{2,0,1:T(8,128)(2,1)S(1)}, u32[]{:S(2)}, u32[]{:S(2)}) collective-permute-start(bf16[96,2,512]{2,0,1:T(8,128)(2,1)S(1)} %get-tuple-element.49), channel_id=1, source_target_pairs={{1,0},{2,1},{3,2},{4,3},{5,4},{6,5},{7,6},{8,7},{9,8},{10,9},{11,1... | collective-permute-start | bytes 589832 | tf_op jit(solution)/shard_map/ppermute | solution.py:24
  55.5 1.8 %collective-permute-done.3 = bf16[96,2,512]{2,0,1:T(8,128)(2,1)S(1)} collective-permute-done((bf16[96,2,512]{2,0,1:T(8,128)(2,1)S(1)}, bf16[96,2,512]{2,0,1:T(8,128)(2,1)S(1)}, u32[]{:S(2)}, u32[]{:S(2)}) %collective-permute-start.3) | collective-permute-done | bytes 196640 | tf_op jit(solution)/shard_map/ppermute | solution.py:24
  57.6 0.8 fusion.45
  58.5 1.1 slice_bitcast_fusion.6
  61.6 0.7 convolution_add_fusion.12
  64.0 32.1 %all-reduce.4 = (f32[96]{0:T(128)S(1)}, f32[96]{0:T(128)S(1)}) all-reduce(f32[96]{0:T(128)S(1)} %get-tuple-element.8, f32[96]{0:T(128)S(1)} %get-tuple-element.7), channel_id=1, replica_groups=mesh['groups'=2,'rows'=16] {'rows'}, use_global_device_ids=true, to_apply=%region_7.8 | all-reduce | flops 192 | bytes 1536 | tf_op jit(solution)/shard_map/psum | solution.py:65
  97.2 1.3 collective-permute-start.4
  98.5 1.5 %collective-permute-start.5 = (bf16[96,4,512]{2,0,1:T(8,128)(2,1)S(1)}, bf16[96,4,512]{2,0,1:T(8,128)(2,1)S(1)}, u32[]{:S(2)}, u32[]{:S(2)}) collective-permute-start(bf16[96,4,512]{2,0,1:T(8,128)(2,1)S(1)} %get-tuple-element.45), channel_id=1, source_target_pairs={{1,0},{2,1},{3,2},{4,3},{5,4},{6,5},{7,6},{8,7},{9,8},{10,9},{11,1... | collective-permute-start | bytes 1179656 | tf_op jit(solution)/shard_map/ppermute | solution.py:24
  100.0 2.1 %collective-permute-done.5 = bf16[96,4,512]{2,0,1:T(8,128)(2,1)S(1)} collective-permute-done((bf16[96,4,512]{2,0,1:T(8,128)(2,1)S(1)}, bf16[96,4,512]{2,0,1:T(8,128)(2,1)S(1)}, u32[]{:S(2)}, u32[]{:S(2)}) %collective-permute-start.5) | collective-permute-done | bytes 393248 | tf_op jit(solution)/shard_map/ppermute | solution.py:24
  102.4 1.1 fusion.7
  103.5 1.3 slice_bitcast_fusion
  106.8 0.7 convolution_add_fusion.4
  109.1 32.9 %all-reduce.3 = (f32[96]{0:T(128)S(1)}, f32[96]{0:T(128)S(1)}) all-reduce(f32[96]{0:T(128)S(1)} %get-tuple-element.6, f32[96]{0:T(128)S(1)} %get-tuple-element.5), channel_id=1, replica_groups=mesh['groups'=2,'rows'=16] {'rows'}, use_global_device_ids=true, to_apply=%region_11.12 | all-reduce | flops 192 | bytes 1536 | tf_op jit(solution)/shard_map/psum | solution.py:65
  143.2 1.3 copy.77
  (85 shorter events, 17.2 us)
Async XLA Ops:
  0.0 0.9 copy-start
  0.0 7.1 %copy-start.2 = (bf16[96,8,512]{2,1,0:T(8,128)(2,1)S(1)}, bf16[96,8,512]{2,1,0:T(8,128)(2,1)}, u32[]{:S(2)}) copy-start(bf16[96,8,512]{2,1,0:T(8,128)(2,1)} %param.7) | copy-start | bytes 2359300
  1.9 5.5 %copy-start.4 = (f32[3,96]{1,0:T(4,128)S(1)}, f32[3,96]{1,0:T(4,128)}, u32[]{:S(2)}) copy-start(f32[3,96]{1,0:T(4,128)} %param.13) | copy-start | bytes 3460
  1.9 5.5 %copy-start.5 = (f32[3,96]{1,0:T(4,128)S(1)}, f32[3,96]{1,0:T(4,128)}, u32[]{:S(2)}) copy-start(f32[3,96]{1,0:T(4,128)} %param.12) | copy-start | bytes 3460
  3.4 4.7 %collective-permute-start = (bf16[96,1,512]{2,0,1:T(8,128)(2,1)S(1)}, bf16[96,1,512]{2,0,1:T(8,128)(2,1)S(1)}, u32[]{:S(2)}, u32[]{:S(2)}) collective-permute-start(bf16[96,1,512]{2,0,1:T(8,128)(2,1)S(1)} %get-tuple-element.52), channel_id=1, source_target_pairs={{0,1},{1,2},{2,3},{3,4},{4,5},{5,6},{6,7},{7,8},{8,9},{9,10},{10,1... | collective-permute-start | bytes 294920 | tf_op jit(solution)/shard_map/ppermute | solution.py:22
  5.8 5.3 %collective-permute-start.1 = (bf16[96,1,512]{2,0,1:T(8,128)(2,1)S(1)}, bf16[96,1,512]{2,0,1:T(8,128)(2,1)S(1)}, u32[]{:S(2)}, u32[]{:S(2)}) collective-permute-start(bf16[96,1,512]{2,0,1:T(8,128)(2,1)S(1)} %get-tuple-element.53), channel_id=1, source_target_pairs={{1,0},{2,1},{3,2},{4,3},{5,4},{6,5},{7,6},{8,7},{9,8},{10,9},{11,1... | collective-permute-start | bytes 294920 | tf_op jit(solution)/shard_map/ppermute | solution.py:24
  13.5 1.1 copy-start.3
  52.7 2.8 %collective-permute-start.2 = (bf16[96,2,512]{2,0,1:T(8,128)(2,1)S(1)}, bf16[96,2,512]{2,0,1:T(8,128)(2,1)S(1)}, u32[]{:S(2)}, u32[]{:S(2)}) collective-permute-start(bf16[96,2,512]{2,0,1:T(8,128)(2,1)S(1)} %get-tuple-element.48), channel_id=1, source_target_pairs={{0,1},{1,2},{2,3},{3,4},{4,5},{5,6},{6,7},{7,8},{8,9},{9,10},{10,1... | collective-permute-start | bytes 589832 | tf_op jit(solution)/shard_map/ppermute | solution.py:22
  54.0 3.3 %collective-permute-start.3 = (bf16[96,2,512]{2,0,1:T(8,128)(2,1)S(1)}, bf16[96,2,512]{2,0,1:T(8,128)(2,1)S(1)}, u32[]{:S(2)}, u32[]{:S(2)}) collective-permute-start(bf16[96,2,512]{2,0,1:T(8,128)(2,1)S(1)} %get-tuple-element.49), channel_id=1, source_target_pairs={{1,0},{2,1},{3,2},{4,3},{5,4},{6,5},{7,6},{8,7},{9,8},{10,9},{11,1... | collective-permute-start | bytes 589832 | tf_op jit(solution)/shard_map/ppermute | solution.py:24
  97.2 2.8 %collective-permute-start.4 = (bf16[96,4,512]{2,0,1:T(8,128)(2,1)S(1)}, bf16[96,4,512]{2,0,1:T(8,128)(2,1)S(1)}, u32[]{:S(2)}, u32[]{:S(2)}) collective-permute-start(bf16[96,4,512]{2,0,1:T(8,128)(2,1)S(1)} %get-tuple-element.44), channel_id=1, source_target_pairs={{0,1},{1,2},{2,3},{3,4},{4,5},{5,6},{6,7},{7,8},{8,9},{9,10},{10,1... | collective-permute-start | bytes 1179656 | tf_op jit(solution)/shard_map/ppermute | solution.py:22
  98.5 3.6 %collective-permute-start.5 = (bf16[96,4,512]{2,0,1:T(8,128)(2,1)S(1)}, bf16[96,4,512]{2,0,1:T(8,128)(2,1)S(1)}, u32[]{:S(2)}, u32[]{:S(2)}) collective-permute-start(bf16[96,4,512]{2,0,1:T(8,128)(2,1)S(1)} %get-tuple-element.45), channel_id=1, source_target_pairs={{1,0},{2,1},{3,2},{4,3},{5,4},{6,5},{7,6},{8,7},{9,8},{10,9},{11,1... | collective-permute-start | bytes 1179656 | tf_op jit(solution)/shard_map/ppermute | solution.py:24
  142.7 1.8 %copy-start.1 = (f32[4,96]{1,0:T(4,128)S(1)}, f32[4,96]{1,0:T(4,128)}, u32[]{:S(2)}) copy-start(f32[4,96]{1,0:T(4,128)} %param.10) | copy-start | bytes 4612
where the time goes:
time: 145 us; the launch traced here: 144 us
  blocking collectives  98.4 us (68%)
  matrix products  11.9 us (8%)
  other arithmetic  9.36 us (6%)
  starting transfers between devices  9.3 us (6%)
  local copies, waits for them, and re-layouts  7.9 us (5%)
  waiting for transfers between devices  6.92 us (5%)
    psum x3, blocking collectives, statistics(): lax.psum((jnp.sum(masked, axis=(1, 2)), jnp.sum(masked * own_response, ax...  98.4 us
    dot_general x27, matrix products, dilated(): jnp.dot(weights[kernel_tap], window.reshape(inputs.shape[0], -1), preferr...  11.1 us
    ppermute x3, waiting for transfers between devices, with_halo(): lax.ppermute(head, axis, [((i + 1) % count, i) for i in range(ends)])  6.91 us
    ppermute x3, starting transfers between devices, with_halo(): lax.ppermute(tail, axis, [(i, (i + 1) % count) for i in range(ends)])  5.02 us
    unnamed x16, local copies, waits for them, and re-layouts  4.42 us
    ppermute x3, starting transfers between devices, with_halo(): lax.ppermute(head, axis, [((i + 1) % count, i) for i in range(ends)])  4.28 us
  transfers between devices with their start and end apart: 6, of which 3 were waited for; matrix products, arithmetic and copies ran while one was open for 1% of the time, Pallas kernels for 0%

commit v1 on v0

v1 whole, which is shorter than its diff:
```python
import functools

import jax
import jax.numpy as jnp
from jax import lax
from jax.experimental import pallas as pl
from jax.experimental.pallas import tpu as pltpu
from jax.sharding import PartitionSpec as P

LAYERS = 3
TILE = 8
STAINS = 4
REACH = 2**LAYERS - 1
EPSILON = 1e-05
MESH = pl.DeviceIdType.MESH


def kernel(
    peers,
    slide_ref,
    flags_ref,
    index_ref,
    stain_ref,
    weights_ref,
    gain_ref,
    bias_ref,
    out_ref,
    turned,
    x0,
    x1,
    x2,
    response,
    taps,
    masks,
    flag_out,
    flag_in,
    tally_out,
    tally_in,
    edge_send,
    edge_recv,
    tally_send,
    tally_recv,
):
    channels, rows, cols = slide_ref.shape
    tiles = flags_ref.shape[1]
    me = lax.axis_index("rows")
    has_up = me > 0
    has_down = me < peers - 1
    inputs = (x0, x1, x2)
    first = (REACH, REACH - 1, REACH - 3)
    base = REACH - 1

    flag_in[...] = jnp.zeros_like(flag_in)
    barrier = pltpu.get_barrier_semaphore()

    def greet(step, carry):
        other = lax.rem(me + step, peers)
        pl.semaphore_signal(barrier, inc=1, device_id={"rows": other}, device_id_type=MESH)
        return carry

    lax.fori_loop(1, peers, greet, 0)

    spread = (
        lax.broadcasted_iota(jnp.int32, (128, cols), 1) // TILE
        == lax.broadcasted_iota(jnp.int32, (128, cols), 0)
    ).astype(jnp.float32)
    eye = lax.broadcasted_iota(jnp.int32, (channels, channels), 0) == lax.broadcasted_iota(
        jnp.int32, (channels, channels), 1
    )

    def column(row):
        return jnp.sum(jnp.where(eye, row, 0.0), axis=1, keepdims=True)

    def as_row(col):
        return jnp.sum(jnp.where(eye, col, 0.0), axis=0, keepdims=True)

    def widen(flags):
        return jnp.dot(flags, spread, preferred_element_type=jnp.float32)

    flag_out[...] = jnp.zeros_like(flag_out)
    flag_out[:, 0:tiles] = jnp.broadcast_to(
        flags_ref[...].astype(jnp.float32), (flag_out.shape[0], tiles)
    )
    masks[0] = widen(flag_out[...])
    classes = jnp.dot(
        jnp.broadcast_to(index_ref[...].astype(jnp.float32), (8, tiles)),
        spread[0:tiles],
        preferred_element_type=jnp.float32,
    )[0:1]
    scale = jnp.zeros((channels, cols), jnp.float32)
    for stain in range(STAINS):
        scale = jnp.where(classes == stain, column(stain_ref[stain : stain + 1, :]), scale)

    chunks = cols // 128
    for at in range(chunks):
        turned[at] = (
            slide_ref[:, :, at * 128 : (at + 1) * 128]
            .astype(jnp.float32)
            .reshape(channels * rows, 128)
        )
    response[0] = scale
    lane = lax.broadcasted_iota(jnp.int32, (1, cols), 1)

    def place(buffer, row, values, spacing):
        buffer[1, row] = values.astype(jnp.bfloat16)
        shifted = pltpu.roll(values, spacing, 1)
        buffer[0, row] = jnp.where(lane >= spacing, shifted, 0.0).astype(jnp.bfloat16)
        shifted = pltpu.roll(values, cols - spacing, 1)
        buffer[2, row] = jnp.where(lane < cols - spacing, shifted, 0.0).astype(jnp.bfloat16)

    def load_row(row, carry):
        values = jnp.concatenate(
            [turned[at, pl.ds(row, channels, stride=rows), :] for at in range(chunks)], axis=1
        )
        values = values * response[0] * masks[0, 0:1, :]
        values = values.astype(jnp.bfloat16).astype(jnp.float32)
        place(x0, first[0] + row, values, 1)
        return carry

    lax.fori_loop(0, rows, load_row, 0)

    @pl.when(jnp.logical_not(has_up))
    def _():
        x0[1, 0:REACH] = jnp.zeros((REACH, channels, cols), jnp.bfloat16)

    @pl.when(jnp.logical_not(has_down))
    def _():
        x0[1, REACH + rows : 2 * REACH + rows] = jnp.zeros((REACH, channels, cols), jnp.bfloat16)

    pl.semaphore_wait(barrier, peers - 1)

    def edge_copy(piece, side):
        if piece == 0:
            source, target = flag_out, flag_in.at[1 - side]
        else:
            lo, count = 2 ** (piece - 1) - 1, 2 ** (piece - 1)
            if side == 0:
                start, land = REACH + lo, REACH + rows + lo
            else:
                start, land = REACH + rows - lo - count, REACH - lo - count
            source, target = x0.at[1, pl.ds(start, count)], x0.at[1, pl.ds(land, count)]
        return pltpu.make_async_remote_copy(
            src_ref=source,
            dst_ref=target,
            send_sem=edge_send.at[piece, side],
            recv_sem=edge_recv.at[piece, side],
            device_id={"rows": me - 1 if side == 0 else me + 1},
            device_id_type=MESH,
        )

    def send_edge(piece):
        @pl.when(has_up)
        def _():
            edge_copy(piece, 0).start()

        @pl.when(has_down)
        def _():
            edge_copy(piece, 1).start()

    def take_edge(piece):
        @pl.when(has_down)
        def _():
            edge_copy(piece, 0).wait_recv()

        @pl.when(has_up)
        def _():
            edge_copy(piece, 1).wait_recv()

    for piece in (1, 0, 2, 3):
        send_edge(piece)

    for layer in range(LAYERS):
        for tap in range(9):
            taps[layer, :, tap * channels : (tap + 1) * channels] = weights_ref[layer, tap]

    def widen_edge(piece):
        lo, count = 2 ** (piece - 1) - 1, 2 ** (piece - 1)
        for start in (REACH - lo - count, REACH + rows + lo):
            def one(row, carry):
                place_shifts(x0, start + row)
                return carry
            lax.fori_loop(0, count, one, 0)

    def place_shifts(buffer, row):
        values = buffer[1, row].astype(jnp.float32)
        shifted = pltpu.roll(values, 1, 1)
        buffer[0, row] = jnp.where(lane >= 1, shifted, 0.0).astype(jnp.bfloat16)
        shifted = pltpu.roll(values, cols - 1, 1)
        buffer[2, row] = jnp.where(lane < cols - 1, shifted, 0.0).astype(jnp.bfloat16)

    def conv_row(layer, row):
        spacing = 2**layer
        source = inputs[layer]
        window = jnp.concatenate(
            [
                source[b, first[layer] + row + (a - 1) * spacing]
                for a in range(3)
                for b in range(3)
            ],
            axis=0,
        )
        return jnp.dot(taps[layer], window, preferred_element_type=jnp.float32)

    def conv_edges(layer, lo, count):
        for start in (-lo - count, rows + lo):
            def one(row, carry):
                response[base + start + row] = conv_row(layer, start + row)
                return carry
            lax.fori_loop(0, count, one, 0)

    def fold(values):
        total = values[:, 0:128]
        for at in range(128, cols, 128):
            total = total + values[:, at : at + 128]
        return total

    def conv_own(layer):
        def one(row, carry):
            sums, squares = carry
            own = conv_row(layer, row)
            response[base + row] = own
            masked = own * masks[0, 0:1, :]
            return sums + fold(masked), squares + fold(masked * own)

        zero = jnp.zeros((channels, 128), jnp.float32)
        sums, squares = lax.fori_loop(0, rows, one, (zero, zero))
        tally_out[layer] = jnp.zeros(tally_out.shape[1:], jnp.float32)
        tally_out[layer, 0:1, 0:channels] = as_row(jnp.sum(sums, axis=1, keepdims=True))
        tally_out[layer, 1:2, 0:channels] = as_row(jnp.sum(squares, axis=1, keepdims=True))
        pixels = jnp.sum(masks[0, 0:1, :], axis=1, keepdims=True) * rows
        tally_out[layer, 2:3, :] = jnp.broadcast_to(pixels, (1, 128))
        tally_in[layer, me] = tally_out[layer]

    def tally_copy(layer, step, other, slot):
        return pltpu.make_async_remote_copy(
            src_ref=tally_out.at[layer],
            dst_ref=tally_in.at[layer, slot],
            send_sem=tally_send.at[layer, step],
            recv_sem=tally_recv.at[layer, slot],
            device_id={"rows": other},
            device_id_type=MESH,
        )

    def send_tally(layer):
        def one(step, carry):
            tally_copy(layer, step, lax.rem(me + step, peers), me).start()
            return carry

        lax.fori_loop(1, peers, one, 0)

    def take_tally(layer):
        def one(step, carry):
            other = lax.rem(me + step, peers)
            tally_copy(layer, step, other, other).wait_recv()
            return carry

        lax.fori_loop(1, peers, one, 0)
        total = jnp.sum(tally_in[layer], axis=0)
        count = total[2:3, 0:channels]
        average = total[0:1, 0:channels] / count
        variance = jnp.maximum(total[1:2, 0:channels] / count - average * average, 0.0)
        factor = gain_ref[layer : layer + 1, :] * lax.rsqrt(variance + EPSILON)
        return column(average), column(factor), column(bias_ref[layer : layer + 1, :])

    def finish_row(row, norm, mask):
        average, factor, bias = norm
        scaled = (response[base + row] - average) * factor + bias
        return jnp.maximum(scaled, 0.0) * masks[mask, 0:1, :]

    def finish(layer, start, count, norm, mask):
        def one(row, carry):
            place(
                inputs[layer + 1],
                first[layer + 1] + start + row,
                finish_row(start + row, norm, mask),
                2 ** (layer + 1),
            )
            return carry

        lax.fori_loop(0, count, one, 0)

    def finish_edges(layer, lo, count, norm):
        finish(layer, -lo - count, count, norm, 1)
        finish(layer, rows + lo, count, norm, 2)

    take_edge(1)
    widen_edge(1)
    conv_own(0)
    send_tally(0)
    take_edge(0)
    masks[1] = widen(flag_in[0])
    masks[2] = widen(flag_in[1])
    take_edge(2)
    widen_edge(2)
    conv_edges(0, 0, 2)
    norm0 = take_tally(0)
    finish(0, 0, rows, norm0, 0)
    finish_edges(0, 0, 2, norm0)
    take_edge(3)
    widen_edge(3)
    conv_edges(0, 2, 4)
    finish_edges(0, 2, 4, norm0)
    conv_own(1)
    send_tally(1)
    conv_edges(1, 0, 4)
    norm1 = take_tally(1)
    finish(1, 0, rows, norm1, 0)
    finish_edges(1, 0, 4, norm1)
    conv_own(2)
    send_tally(2)
    norm2 = take_tally(2)

    def last(row, carry):
        values = finish_row(row, norm2, 0)
        for at in range(chunks):
            turned[at, pl.ds(row, channels, stride=rows), :] = values[:, at * 128 : (at + 1) * 128]
        return carry

    lax.fori_loop(0, rows, last, 0)
    for at in range(chunks):
        out_ref[:, :, at * 128 : (at + 1) * 128] = (
            turned[at].reshape(channels, rows, 128).astype(out_ref.dtype)
        )

    for piece in range(4):
        @pl.when(has_up)
        def _():
            edge_copy(piece, 0).wait_send()

        @pl.when(has_down)
        def _():
            edge_copy(piece, 1).wait_send()

    for layer in range(LAYERS):
        def one(step, carry):
            tally_copy(layer, step, lax.rem(me + step, peers), me).wait_send()
            return carry

        lax.fori_loop(1, peers, one, 0)


def per_device(peers, *arrays):
    channels, rows, cols = arrays[0].shape
    assert rows == TILE and rows > REACH and arrays[1].shape[0] == 1
    f32, bf16 = jnp.float32, jnp.bfloat16
    vmem = pl.BlockSpec(memory_space=pltpu.VMEM)
    return pl.pallas_call(
        functools.partial(kernel, peers),
        out_shape=jax.ShapeDtypeStruct((channels, rows, cols), bf16),
        in_specs=[vmem] * 7,
        out_specs=vmem,
        scratch_shapes=[
            pltpu.VMEM((cols // 128, channels * rows, 128), f32),
            pltpu.VMEM((3, rows + 2 * REACH, channels, cols), bf16),
            pltpu.VMEM((3, rows + 2 * (REACH - 1), channels, cols), bf16),
            pltpu.VMEM((3, rows + 2 * (REACH - 3), channels, cols), bf16),
            pltpu.VMEM((rows + 2 * (REACH - 1), channels, cols), f32),
            pltpu.VMEM((LAYERS, channels, 9 * channels), bf16),
            pltpu.VMEM((3, 8, cols), f32),
            pltpu.VMEM((8, 128), f32),
            pltpu.VMEM((2, 8, 128), f32),
            pltpu.VMEM((LAYERS, 8, 128), f32),
            pltpu.VMEM((LAYERS, peers, 8, 128), f32),
            pltpu.SemaphoreType.DMA((4, 2)),
            pltpu.SemaphoreType.DMA((4, 2)),
            pltpu.SemaphoreType.DMA((LAYERS, peers)),
            pltpu.SemaphoreType.DMA((LAYERS, peers)),
        ],
        compiler_params=pltpu.CompilerParams(
            collective_id=0, has_side_effects=True, vmem_limit_bytes=56 * 2**20
        ),
    )(*arrays)


def solution(mesh):
    banded = P(None, ("groups", "rows"), None)
    tiled = P(("groups", "rows"), None)
    return jax.shard_map(
        functools.partial(per_device, mesh.shape["rows"]),
        mesh=mesh,
        in_specs=(banded, tiled, tiled, P(), P(), P(), P()),
        out_specs=banded,
        check_vma=False,
    )
```

time: 145 us -> 52.2 us (0.36)
  blocking collectives: 98.4 us -> 0 us
  Pallas kernels: 0 us -> 49.9 us
  matrix products: 11.9 us -> 0 us
  other arithmetic: 9.36 us -> 0 us
  starting transfers between devices: 9.3 us -> 0 us
  waiting for transfers between devices: 6.92 us -> 0 us
  local copies, waits for them, and re-layouts: 7.9 us -> 2.06 us
    psum x3 -> x0, blocking collectives: 98.4 us -> none  [statistics(): lax.psum((jnp.sum(masked, axis=(1, 2)), jnp.sum(masked * own_response, ax...]
    pallas_call x0 -> x1, Pallas kernels: none -> 49.9 us  [per_device(): pl.pallas_call(functools.partial(kernel, peers), out_shape=jax.ShapeDtype...]
    dot_general x28 -> x0, matrix products: 11.9 us -> none  [the longest x27 11.1 us: dilated(): jnp.dot(weights[kernel_tap], window.reshape(inputs.shape[0], -1), preferr...]
    ppermute x6 -> x0, starting transfers between devices: 9.3 us -> none  [the longest x3 5.02 us: with_halo(): lax.ppermute(tail, axis, [(i, (i + 1) % count) for i in range(ends)])]
    ppermute x6 -> x0, waiting for transfers between devices: 6.92 us -> none  [the longest x3 6.91 us: with_halo(): lax.ppermute(head, axis, [((i + 1) % count, i) for i in range(ends)])]
    convert_element_type x4 -> x0, other arithmetic: 2.77 us -> none  [the longest x1 1.44 us: per_device(): (slide_band.astype(jnp.float32) * stain_scale * pixels[None]).astype(jnp....]
    concatenate x3 -> x0, other arithmetic: 2.6 us -> none  [with_halo(): jnp.concatenate([lax.ppermute(tail, axis, [(i, (i + 1) % count) for i in...]
    unnamed x16 -> x1, local copies, waits for them, and re-layouts: 4.42 us -> 2.06 us
  transfers between devices with their start and end apart: 6 -> 0, of which waited for: 3 -> 0; matrix products, arithmetic and copies ran while one was open for 1% -> 0% of each run, Pallas kernels for 0% -> 0%
where the time goes in v1:
time: 52.2 us; the launch traced here: 52 us
  Pallas kernels  49.9 us (96%)
  local copies, waits for them, and re-layouts  2.06 us (4%)
    pallas_call x1, Pallas kernels, per_device(): pl.pallas_call(functools.partial(kernel, peers), out_shape=jax.ShapeDtype...  49.9 us
    unnamed x1, local copies, waits for them, and re-layouts  2.06 us

profile of v1, /device:TPU:0, one launch (start us, length us, event | category | flops | bytes accessed | tf_op | source)
XLA Modules:
  0.0 52.0 jit_solution(10975168452605066314)
XLA Ops:
  0.0 49.9 %shard_map.73 = bf16[96,8,512]{2,1,0:T(8,128)(2,1)} custom-call(bf16[96,8,512]{2,1,0:T(8,128)(2,1)} %slide_ref.1, s32[1,64]{1,0:T(1,128)} %flags_ref.1, s32[1,64]{1,0:T(1,128)} %index_ref.1, f32[4,96]{1,0:T(4,128)} %stain_ref.1, bf16[3,9,96,96]{3,2,1,0:T(8,128)(2,1)} %weights_ref.1, f32[3,96]{1,0:T(4,128)} %gain_ref.1, f32[3,96]{1,0:T(4,128)} %bias_ref.1), custom_call_target="tpu_custom_call" | custom-call | tf_op jit(solution)/shard_map/pallas_call | solution.py:347
  49.9 2.1 %copy.9 = bf16[96,8,512]{2,1,0:T(8,128)(2,1)} copy(bf16[96,8,512]{2,1,0:T(8,128)(2,1)} %shard_map.73) | data formatting | bytes 1572864

commit v2 on v1

--- a/solution.py
+++ b/solution.py
@@ -25,6 +25,9 @@
     gain_ref,
     bias_ref,
     out_ref,
+    slide,
+    weights,
+    result,
     turned,
     x0,
     x1,
@@ -40,6 +43,7 @@
     edge_recv,
     tally_send,
     tally_recv,
+    local_sem,
 ):
     channels, rows, cols = slide_ref.shape
     tiles = flags_ref.shape[1]
@@ -59,6 +63,20 @@
         return carry
 
     lax.fori_loop(1, peers, greet, 0)
+    slide_copy = pltpu.make_async_copy(slide_ref, slide, local_sem.at[0])
+    slide_copy.start()
+    weights_copy = pltpu.make_async_copy(weights_ref, weights, local_sem.at[1])
+    weights_copy.start()
+
+    def loop(count, one):
+        width = 2 if count % 2 == 0 else 1
+
+        def several(step, carry):
+            for k in range(width):
+                one(step * width + k)
+            return carry
+
+        lax.fori_loop(0, count // width, several, 0)
 
     spread = (
         lax.broadcasted_iota(jnp.int32, (128, cols), 1) // TILE
@@ -92,9 +110,10 @@
         scale = jnp.where(classes == stain, column(stain_ref[stain : stain + 1, :]), scale)
 
     chunks = cols // 128
+    slide_copy.wait()
     for at in range(chunks):
         turned[at] = (
-            slide_ref[:, :, at * 128 : (at + 1) * 128]
+            slide[:, :, at * 128 : (at + 1) * 128]
             .astype(jnp.float32)
             .reshape(channels * rows, 128)
         )
@@ -108,16 +127,15 @@
         shifted = pltpu.roll(values, cols - spacing, 1)
         buffer[2, row] = jnp.where(lane < cols - spacing, shifted, 0.0).astype(jnp.bfloat16)
 
-    def load_row(row, carry):
+    def load_row(row):
         values = jnp.concatenate(
             [turned[at, pl.ds(row, channels, stride=rows), :] for at in range(chunks)], axis=1
         )
         values = values * response[0] * masks[0, 0:1, :]
         values = values.astype(jnp.bfloat16).astype(jnp.float32)
         place(x0, first[0] + row, values, 1)
-        return carry
-
-    lax.fori_loop(0, rows, load_row, 0)
+
+    loop(rows, load_row)
 
     @pl.when(jnp.logical_not(has_up))
     def _():
@@ -166,20 +184,18 @@
         def _():
             edge_copy(piece, 1).wait_recv()
 
-    for piece in (1, 0, 2, 3):
+    for piece in (1, 0, 2):
         send_edge(piece)
 
+    weights_copy.wait()
     for layer in range(LAYERS):
         for tap in range(9):
-            taps[layer, :, tap * channels : (tap + 1) * channels] = weights_ref[layer, tap]
+            taps[layer, :, tap * channels : (tap + 1) * channels] = weights[layer, tap]
 
     def widen_edge(piece):
         lo, count = 2 ** (piece - 1) - 1, 2 ** (piece - 1)
         for start in (REACH - lo - count, REACH + rows + lo):
-            def one(row, carry):
-                place_shifts(x0, start + row)
-                return carry
-            lax.fori_loop(0, count, one, 0)
+            loop(count, lambda row: place_shifts(x0, start + row))
 
     def place_shifts(buffer, row):
         values = buffer[1, row].astype(jnp.float32)
@@ -203,10 +219,11 @@
 
     def conv_edges(layer, lo, count):
         for start in (-lo - count, rows + lo):
-            def one(row, carry):
+
+            def one(row):
                 response[base + start + row] = conv_row(layer, start + row)
-                return carry
-            lax.fori_loop(0, count, one, 0)
+
+            loop(count, one)
 
     def fold(values):
         total = values[:, 0:128]
@@ -214,16 +231,23 @@
             total = total + values[:, at : at + 128]
         return total
 
-    def conv_own(layer):
-        def one(row, carry):
-            sums, squares = carry
-            own = conv_row(layer, row)
-            response[base + row] = own
-            masked = own * masks[0, 0:1, :]
-            return sums + fold(masked), squares + fold(masked * own)
-
-        zero = jnp.zeros((channels, 128), jnp.float32)
-        sums, squares = lax.fori_loop(0, rows, one, (zero, zero))
+    def own_row(layer, row, carry):
+        sums, squares = carry
+        own = conv_row(layer, row)
+        response[base + row] = own
+        masked = own * masks[0, 0:1, :]
+        return sums + fold(masked), squares + fold(masked * own)
+
+    def own_rows(layer, start, count, carry):
+        def two(step, carry):
+            for k in range(2):
+                carry = own_row(layer, start + 2 * step + k, carry)
+            return carry
+
+        return lax.fori_loop(0, count // 2, two, carry)
+
+    def tally(layer, carry):
+        sums, squares = carry
         tally_out[layer] = jnp.zeros(tally_out.shape[1:], jnp.float32)
         tally_out[layer, 0:1, 0:channels] = as_row(jnp.sum(sums, axis=1, keepdims=True))
         tally_out[layer, 1:2, 0:channels] = as_row(jnp.sum(squares, axis=1, keepdims=True))
@@ -268,25 +292,29 @@
         return jnp.maximum(scaled, 0.0) * masks[mask, 0:1, :]
 
     def finish(layer, start, count, norm, mask):
-        def one(row, carry):
+        def one(row):
             place(
                 inputs[layer + 1],
                 first[layer + 1] + start + row,
                 finish_row(start + row, norm, mask),
                 2 ** (layer + 1),
             )
-            return carry
-
-        lax.fori_loop(0, count, one, 0)
+
+        loop(count, one)
 
     def finish_edges(layer, lo, count, norm):
         finish(layer, -lo - count, count, norm, 1)
         finish(layer, rows + lo, count, norm, 2)
 
+    nothing = jnp.zeros((channels, 128), jnp.float32)
+    nothing = (nothing, nothing)
+
+    inner = own_rows(0, 1, rows - 2, nothing)
     take_edge(1)
     widen_edge(1)
-    conv_own(0)
+    tally(0, own_row(0, rows - 1, own_row(0, 0, inner)))
     send_tally(0)
+    send_edge(3)
     take_edge(0)
     masks[1] = widen(flag_in[0])
     masks[2] = widen(flag_in[1])
@@ -296,31 +324,32 @@
     norm0 = take_tally(0)
     finish(0, 0, rows, norm0, 0)
     finish_edges(0, 0, 2, norm0)
+    tally(1, own_rows(1, 0, rows, nothing))
+    send_tally(1)
     take_edge(3)
     widen_edge(3)
     conv_edges(0, 2, 4)
     finish_edges(0, 2, 4, norm0)
-    conv_own(1)
-    send_tally(1)
     conv_edges(1, 0, 4)
     norm1 = take_tally(1)
     finish(1, 0, rows, norm1, 0)
     finish_edges(1, 0, 4, norm1)
-    conv_own(2)
+    tally(2, own_rows(2, 0, rows, nothing))
     send_tally(2)
     norm2 = take_tally(2)
 
-    def last(row, carry):
+    def last(row):
         values = finish_row(row, norm2, 0)
         for at in range(chunks):
             turned[at, pl.ds(row, channels, stride=rows), :] = values[:, at * 128 : (at + 1) * 128]
-        return carry
-
-    lax.fori_loop(0, rows, last, 0)
+
+    loop(rows, last)
     for at in range(chunks):
-        out_ref[:, :, at * 128 : (at + 1) * 128] = (
-            turned[at].reshape(channels, rows, 128).astype(out_ref.dtype)
-        )
+        result[:, :, at * 128 : (at + 1) * 128] = (
+            turned[at].reshape(channels, rows, 128).astype(result.dtype)
+        )
+    result_copy = pltpu.make_async_copy(result, out_ref, local_sem.at[2])
+    result_copy.start()
 
     for piece in range(4):
         @pl.when(has_up)
@@ -337,6 +366,8 @@
             return carry
 
         lax.fori_loop(1, peers, one, 0)
+
+    result_copy.wait()
 
 
 def per_device(peers, *arrays):
@@ -344,12 +375,16 @@
     assert rows == TILE and rows > REACH and arrays[1].shape[0] == 1
     f32, bf16 = jnp.float32, jnp.bfloat16
     vmem = pl.BlockSpec(memory_space=pltpu.VMEM)
+    hbm = pl.BlockSpec(memory_space=pl.ANY)
     return pl.pallas_call(
         functools.partial(kernel, peers),
         out_shape=jax.ShapeDtypeStruct((channels, rows, cols), bf16),
-        in_specs=[vmem] * 7,
-        out_specs=vmem,
+        in_specs=[hbm, vmem, vmem, vmem, hbm, vmem, vmem],
+        out_specs=hbm,
         scratch_shapes=[
+            pltpu.VMEM((channels, rows, cols), bf16),
+            pltpu.VMEM(arrays[4].shape, bf16),
+            pltpu.VMEM((channels, rows, cols), bf16),
             pltpu.VMEM((cols // 128, channels * rows, 128), f32),
             pltpu.VMEM((3, rows + 2 * REACH, channels, cols), bf16),
             pltpu.VMEM((3, rows + 2 * (REACH - 1), channels, cols), bf16),
@@ -365,6 +400,7 @@
             pltpu.SemaphoreType.DMA((4, 2)),
             pltpu.SemaphoreType.DMA((LAYERS, peers)),
             pltpu.SemaphoreType.DMA((LAYERS, peers)),
+            pltpu.SemaphoreType.DMA((3,)),
         ],
         compiler_params=pltpu.CompilerParams(
             collective_id=0, has_side_effects=True, vmem_limit_bytes=56 * 2**20

time: 52.2 us -> 41.2 us (0.79)
  Pallas kernels: 49.9 us -> 39 us
    pallas_call x1, Pallas kernels: 49.9 us -> 39 us  [per_device(): pl.pallas_call(functools.partial(kernel, peers), out_shape=jax.ShapeDtype...]
where the time goes in v2:
time: 41.2 us; the launch traced here: 41 us
  Pallas kernels  39 us (95%)
  local copies, waits for them, and re-layouts  2.06 us (5%)
    pallas_call x1, Pallas kernels, per_device(): pl.pallas_call(functools.partial(kernel, peers), out_shape=jax.ShapeDtype...  39 us
    unnamed x1, local copies, waits for them, and re-layouts  2.06 us

profile of v2, /device:TPU:0, one launch (start us, length us, event | category | flops | bytes accessed | tf_op | source)
XLA Modules:
  0.0 41.0 jit_solution(10768646713260015034)
XLA Ops:
  0.0 39.0 %shard_map.73 = bf16[96,8,512]{2,1,0:T(8,128)(2,1)} custom-call(bf16[96,8,512]{2,1,0:T(8,128)(2,1)} %slide_ref.1, s32[1,64]{1,0:T(1,128)} %flags_ref.1, s32[1,64]{1,0:T(1,128)} %index_ref.1, f32[4,96]{1,0:T(4,128)} %stain_ref.1, bf16[3,9,96,96]{3,2,1,0:T(8,128)(2,1)} %weights_ref.1, f32[3,96]{1,0:T(4,128)} %gain_ref.1, f32[3,96]{1,0:T(4,128)} %bias_ref.1), custom_call_target="tpu_custom_call" | custom-call | tf_op jit(solution)/shard_map/pallas_call | solution.py:379
  39.0 2.1 %copy.9 = bf16[96,8,512]{2,1,0:T(8,128)(2,1)} copy(bf16[96,8,512]{2,1,0:T(8,128)(2,1)} %shard_map.73) | data formatting | bytes 1572864

commit v3 on v2

--- a/solution.py
+++ b/solution.py
@@ -147,11 +147,13 @@
 
     pl.semaphore_wait(barrier, peers - 1)
 
+    pieces = {1: (0, 1), 2: (1, 2), 3: (3, 2), 4: (5, 2)}
+
     def edge_copy(piece, side):
         if piece == 0:
             source, target = flag_out, flag_in.at[1 - side]
         else:
-            lo, count = 2 ** (piece - 1) - 1, 2 ** (piece - 1)
+            lo, count = pieces[piece]
             if side == 0:
                 start, land = REACH + lo, REACH + rows + lo
             else:
@@ -193,7 +195,7 @@
             taps[layer, :, tap * channels : (tap + 1) * channels] = weights[layer, tap]
 
     def widen_edge(piece):
-        lo, count = 2 ** (piece - 1) - 1, 2 ** (piece - 1)
+        lo, count = pieces[piece]
         for start in (REACH - lo - count, REACH + rows + lo):
             loop(count, lambda row: place_shifts(x0, start + row))
 
@@ -248,11 +250,10 @@
 
     def tally(layer, carry):
         sums, squares = carry
-        tally_out[layer] = jnp.zeros(tally_out.shape[1:], jnp.float32)
         tally_out[layer, 0:1, 0:channels] = as_row(jnp.sum(sums, axis=1, keepdims=True))
         tally_out[layer, 1:2, 0:channels] = as_row(jnp.sum(squares, axis=1, keepdims=True))
         pixels = jnp.sum(masks[0, 0:1, :], axis=1, keepdims=True) * rows
-        tally_out[layer, 2:3, :] = jnp.broadcast_to(pixels, (1, 128))
+        tally_out[layer, :, channels:] = jnp.broadcast_to(pixels, (2, 128 - channels))
         tally_in[layer, me] = tally_out[layer]
 
     def tally_copy(layer, step, other, slot):
@@ -266,8 +267,17 @@
         )
 
     def send_tally(layer):
-        def one(step, carry):
-            tally_copy(layer, step, lax.rem(me + step, peers), me).start()
+        def one(turn, carry):
+            step = peers - turn
+
+            @pl.when(me + step < peers)
+            def _():
+                tally_copy(layer, step, me + step, me).start()
+
+            @pl.when(me >= step)
+            def _():
+                tally_copy(layer, peers - step, me - step, me).start()
+
             return carry
 
         lax.fori_loop(1, peers, one, 0)
@@ -280,7 +290,7 @@
 
         lax.fori_loop(1, peers, one, 0)
         total = jnp.sum(tally_in[layer], axis=0)
-        count = total[2:3, 0:channels]
+        count = total[0:1, channels : channels + 1]
         average = total[0:1, 0:channels] / count
         variance = jnp.maximum(total[1:2, 0:channels] / count - average * average, 0.0)
         factor = gain_ref[layer : layer + 1, :] * lax.rsqrt(variance + EPSILON)
@@ -315,6 +325,7 @@
     tally(0, own_row(0, rows - 1, own_row(0, 0, inner)))
     send_tally(0)
     send_edge(3)
+    send_edge(4)
     take_edge(0)
     masks[1] = widen(flag_in[0])
     masks[2] = widen(flag_in[1])
@@ -326,11 +337,12 @@
     finish_edges(0, 0, 2, norm0)
     tally(1, own_rows(1, 0, rows, nothing))
     send_tally(1)
-    take_edge(3)
-    widen_edge(3)
-    conv_edges(0, 2, 4)
-    finish_edges(0, 2, 4, norm0)
-    conv_edges(1, 0, 4)
+    for piece, lo in ((3, 2), (4, 4)):
+        take_edge(piece)
+        widen_edge(piece)
+        conv_edges(0, lo, 2)
+        finish_edges(0, lo, 2, norm0)
+        conv_edges(1, lo - 2, 2)
     norm1 = take_tally(1)
     finish(1, 0, rows, norm1, 0)
     finish_edges(1, 0, 4, norm1)
@@ -351,7 +363,7 @@
     result_copy = pltpu.make_async_copy(result, out_ref, local_sem.at[2])
     result_copy.start()
 
-    for piece in range(4):
+    for piece in range(5):
         @pl.when(has_up)
         def _():
             edge_copy(piece, 0).wait_send()
@@ -372,7 +384,7 @@
 
 def per_device(peers, *arrays):
     channels, rows, cols = arrays[0].shape
-    assert rows == TILE and rows > REACH and arrays[1].shape[0] == 1
+    assert rows == TILE and rows > REACH and arrays[1].shape[0] == 1 and channels < 128
     f32, bf16 = jnp.float32, jnp.bfloat16
     vmem = pl.BlockSpec(memory_space=pltpu.VMEM)
     hbm = pl.BlockSpec(memory_space=pl.ANY)
@@ -394,10 +406,10 @@
             pltpu.VMEM((3, 8, cols), f32),
             pltpu.VMEM((8, 128), f32),
             pltpu.VMEM((2, 8, 128), f32),
-            pltpu.VMEM((LAYERS, 8, 128), f32),
-            pltpu.VMEM((LAYERS, peers, 8, 128), f32),
-            pltpu.SemaphoreType.DMA((4, 2)),
-            pltpu.SemaphoreType.DMA((4, 2)),
+            pltpu.VMEM((LAYERS, 2, 128), f32),
+            pltpu.VMEM((LAYERS, peers, 2, 128), f32),
+            pltpu.SemaphoreType.DMA((5, 2)),
+            pltpu.SemaphoreType.DMA((5, 2)),
             pltpu.SemaphoreType.DMA((LAYERS, peers)),
             pltpu.SemaphoreType.DMA((LAYERS, peers)),
             pltpu.SemaphoreType.DMA((3,)),

time: 41.2 us -> 40.2 us (0.976)
  Pallas kernels: 39 us -> 38 us
    pallas_call x1, Pallas kernels: 39 us -> 38 us  [per_device(): pl.pallas_call(functools.partial(kernel, peers), out_shape=jax.ShapeDtype...]
where the time goes in v3:
time: 40.2 us; the launch traced here: 40 us
  Pallas kernels  38 us (95%)
  local copies, waits for them, and re-layouts  2.06 us (5%)
    pallas_call x1, Pallas kernels, per_device(): pl.pallas_call(functools.partial(kernel, peers), out_shape=jax.ShapeDtype...  38 us
    unnamed x1, local copies, waits for them, and re-layouts  2.06 us

profile of v3, /device:TPU:0, one launch (start us, length us, event | category | flops | bytes accessed | tf_op | source)
XLA Modules:
  0.0 40.0 jit_solution(15233804473726966501)
XLA Ops:
  0.0 38.0 %shard_map.73 = bf16[96,8,512]{2,1,0:T(8,128)(2,1)} custom-call(bf16[96,8,512]{2,1,0:T(8,128)(2,1)} %slide_ref.1, s32[1,64]{1,0:T(1,128)} %flags_ref.1, s32[1,64]{1,0:T(1,128)} %index_ref.1, f32[4,96]{1,0:T(4,128)} %stain_ref.1, bf16[3,9,96,96]{3,2,1,0:T(8,128)(2,1)} %weights_ref.1, f32[3,96]{1,0:T(4,128)} %gain_ref.1, f32[3,96]{1,0:T(4,128)} %bias_ref.1), custom_call_target="tpu_custom_call" | custom-call | tf_op jit(solution)/shard_map/pallas_call | solution.py:391
  38.0 2.1 %copy.9 = bf16[96,8,512]{2,1,0:T(8,128)(2,1)} copy(bf16[96,8,512]{2,1,0:T(8,128)(2,1)} %shard_map.73) | data formatting | bytes 1572864
